TPU v7x, 32 devices: a whole 2x2x4 slice. The times are simulated.
32 devices in a mesh: expert: 4 (over y, core), mp: 8 (over z, x).
Axes of the slice: x: 2, y: 2, z: 4, core: 2. Of those that a mesh axis runs over, the one named last changes fastest.
Arguments:
- tokens: bfloat16 [512, 6144], P(('expert', 'mp')), may hold values from -18 to 18
- norm_gain: bfloat16 [6144], replicated, may hold values from 0.099609375 to 1.8984375
- expert_ids: int32 [512, 2], P(('expert', 'mp')), may hold values from 0 to 3, as said below
- slot_ids: int32 [512, 2], P(('expert', 'mp')), may hold values from 0 to 7, as said below
- route_weights: float32 [512, 2], P(('expert', 'mp')), may hold values from 0.1 to 1
- w_gate: bfloat16 [4, 6144, 8192], P('expert', None, 'mp'), may hold values from -0.078125 to 0.078125
- w_up: bfloat16 [4, 6144, 8192], P('expert', None, 'mp'), may hold values from -0.078125 to 0.078125
- w_down: bfloat16 [4, 8192, 6144], P('expert', 'mp'), may hold values from -0.0625 to 0.0625
Outputs:
- moe_out: bfloat16 [512, 6144], P(('expert', 'mp'))
Inputs may be any that keep to these rules, and one draw needn't show every extreme that they name: `expert_ids`: each token names two different experts. Among the 16 tokens of one device (aligned blocks of rows) no expert is named more than 8 times, and on every device some expert is named exactly 8 times. `slot_ids`: within the tokens of one device, the entries that name the same expert have different slots; slots that no entry names stay empty.
All inputs are finite; a program needn't handle non-finite values.
Results may differ from a plain program's by a relative error of at most 0.015.
Values may be sent and summed in bfloat16 or wider, within the bound.
A program may use at most 128 MiB of HBM per device.

v0:
```python
import jax
import jax.numpy as jnp
from jax import lax
from jax.sharding import PartitionSpec as P

CAP = 8


def local(tokens, norm_gain, expert_ids, slot_ids, route_weights, w_gate, w_up, w_down):
    tok_rows = tokens.shape[0]
    features = tokens.shape[1]
    experts = w_gate.shape[0] * lax.axis_size("expert")
    values = tokens.astype(jnp.float32)
    mean_square = jnp.mean(values * values, axis=1, keepdims=True)
    normed = (values * lax.rsqrt(mean_square + 1e-05) * norm_gain.astype(jnp.float32)).astype(
        jnp.bfloat16
    )
    target = expert_ids * CAP + slot_ids
    places = lax.broadcasted_iota(jnp.int32, (experts * CAP, tok_rows, 2), 0)
    placing = jnp.any(places == target[None, :, :], axis=2).astype(jnp.bfloat16)
    outgoing = jnp.dot(placing, normed, preferred_element_type=jnp.float32).astype(jnp.bfloat16)
    outgoing = outgoing.reshape(experts, CAP, features)
    gate_local = w_gate[0]
    up_local = w_up[0]
    down_local = w_down[0]
    arrived = lax.all_to_all(outgoing, "expert", split_axis=0, concat_axis=0, tiled=True)
    piece = lax.all_gather(arrived.reshape(experts * CAP, features), "mp", axis=0, tiled=True)
    gate_proj = jnp.dot(piece, gate_local, preferred_element_type=jnp.float32)
    up_proj = jnp.dot(piece, up_local, preferred_element_type=jnp.float32)
    hidden = (jax.nn.silu(gate_proj) * up_proj).astype(jnp.bfloat16)
    piece = hidden
    summed = lax.psum_scatter(
        jnp.dot(piece, down_local, preferred_element_type=jnp.float32).astype(jnp.bfloat16),
        "mp",
        scatter_dimension=0,
        tiled=True,
    )
    results = summed.reshape(experts, CAP, features)
    returned = lax.all_to_all(results, "expert", split_axis=0, concat_axis=0, tiled=True)
    flattened = returned.reshape(experts * CAP, features)
    picked = flattened[target].astype(jnp.float32)
    shares = route_weights / (route_weights[:, 0:1] + route_weights[:, 1:2])
    mixed = jnp.sum(shares[:, :, None] * picked, axis=1)
    return mixed.astype(jnp.bfloat16)


def solution(mesh):
    placed = (
        P(("expert", "mp"), None),
        P(),
        P(("expert", "mp"), None),
        P(("expert", "mp"), None),
        P(("expert", "mp"), None),
        P("expert", None, "mp"),
        P("expert", None, "mp"),
        P("expert", "mp", None),
    )
    return jax.shard_map(
        local, mesh=mesh, in_specs=placed, out_specs=P(("expert", "mp"), None), check_vma=False
    )
```

profile of v0, /device:TPU:0, one launch (start us, length us, event | category | flops | bytes accessed | tf_op | source)
XLA Modules:
  0.0 203.9 jit_solution(15964575743385824110)
XLA Ops:
  6.5 0.0 all-gather.2.cloned.1.call-start
  6.5 0.7 compare_select_fusion
  7.2 0.1 fusion.22
  7.3 0.7 convert_element_type.26
  8.0 1.1 fusion.16
  9.1 1.2 fusion.9
  10.4 11.6 %all_to_all.10 = bf16[4,8,6144]{2,1,0:T(8,128)(2,1)} all-to-all(bf16[4,8,6144]{2,1,0:T(8,128)(2,1)S(1)} %fusion.9), channel_id=1, replica_groups=mesh['expert'=4,'mp'=8] {'expert'}, dimensions={0} | all-to-all | bytes 786432 | tf_op jit(solution)/shard_map/all_to_all | solution.py:26
  22.0 0.0 all-gather.2.cloned.1.call-update
  22.0 0.0 reduce-scatter.2.cloned.1.call-start
  22.0 60.8 %all-gather.2.cloned.1.call-done = bf16[256,6144]{1,0:T(8,128)(2,1)} async-done(((bf16[32,6144]{1,0:T(8,128)(2,1)}), bf16[256,6144]{1,0:T(8,128)(2,1)}) %all-gather.2.cloned.1.call-update) | async-done | bytes 3145744 | tf_op jit(solution)/shard_map/all_gather | solution.py:27
  82.8 0.0 copy-start.1
  82.8 10.1 %fusion.4 = f32[256,1024]{1,0:T(8,128)} fusion(bf16[256,6144]{1,0:T(8,128)(2,1)} %all-gather.2.cloned.1.call-done, bf16[1,6144,1024]{2,1,0:T(8,128)(2,1)} %param.13), kind=kOutput, calls=%fused_computation.5 | convolution fusion | flops 3221225472 | bytes 16777216 | tf_op jit(solution)/shard_map/dot_general | solution.py:28
  92.9 0.0 copy-done.1
  92.9 0.0 copy-start
  92.9 17.0 %fusion.6 = bf16[256,6144]{1,0:T(8,128)(2,1)} fusion(bf16[1,1024,6144]{2,1,0:T(8,128)(2,1)} %param.15, bf16[256,6144]{1,0:T(8,128)(2,1)S(1)} %copy-done.1, bf16[1,6144,1024]{2,1,0:T(8,128)(2,1)} %param.14, f32[256,1024]{1,0:T(8,128)} %fusion.4), kind=kOutput, calls=%fused_computation.7 | convolution fusion | flops 6445596672 | bytes 32505856 | tf_op jit(solution)/shard_map/dot_general | solution.py:33
  109.9 0.0 reduce-scatter.2.cloned.1.call-update
  109.9 0.1 copy.16
  110.0 0.1 reshape.29
  110.1 0.0 copy-done
  110.1 73.0 %reduce-scatter.2.cloned.1.call-done = bf16[32,6144]{1,0:T(8,128)(2,1)} async-done(((bf16[256,6144]{1,0:T(8,128)(2,1)}), bf16[32,6144]{1,0:T(8,128)(2,1)}) %reduce-scatter.2.cloned.1.call-update) | async-done | bytes 393232 | tf_op jit(solution)/shard_map/reduce_scatter | solution.py:32
  183.1 3.5 %all-to-all-start.1 = ((bf16[4,8,6144]{2,1,0:T(8,128)(2,1)}), bf16[4,8,6144]{2,1,0:T(8,128)(2,1)S(1)}, u32[]{:S(2)}, u32[]{:S(2)}) async-start(bf16[4,8,6144]{2,1,0:T(8,128)(2,1)} %bitcast.36), calls=%async_computation.2 | async-start | bytes 786432 | tf_op jit(solution)/shard_map/all_to_all | solution.py:39
  186.6 0.1 copy.15
  186.7 7.3 %all-to-all-done.1 = bf16[4,8,6144]{2,1,0:T(8,128)(2,1)S(1)} async-done(((bf16[4,8,6144]{2,1,0:T(8,128)(2,1)}), bf16[4,8,6144]{2,1,0:T(8,128)(2,1)S(1)}, u32[]{:S(2)}, u32[]{:S(2)}) %all-to-all-start.1) | async-done | bytes 393248 | tf_op jit(solution)/shard_map/all_to_all | solution.py:39
  194.0 0.8 gather_fusion
  194.8 0.5 reshape.37
  195.3 1.7 multiply_reduce_fusion
  (4 shorter events, 0.0 us)
Async XLA Ops:
  6.5 76.3 %all-gather.2.cloned.1.call-start = ((), (), s32[]{:S(2)}) async-start(), calls=%async_computation.3 | async-start | bytes 3538944 | tf_op jit(solution)/shard_map/all_gather | solution.py:27
  22.0 161.2 %reduce-scatter.2.cloned.1.call-start = ((), (), s32[]{:S(2)}) async-start(), calls=%async_computation.4 | async-start | bytes 3538944 | tf_op jit(solution)/shard_map/reduce_scatter | solution.py:32
  82.8 10.1 %copy-start.1 = (bf16[256,6144]{1,0:T(8,128)(2,1)S(1)}, bf16[256,6144]{1,0:T(8,128)(2,1)}, u32[]{:S(2)}) copy-start(bf16[256,6144]{1,0:T(8,128)(2,1)} %all-gather.2.cloned.1.call-done) | copy-start | bytes 9437188
  92.9 17.2 %copy-start = (f32[16,2]{0,1:T(2,128)S(1)}, f32[16,2]{0,1:T(2,128)}, u32[]{:S(2)}) copy-start(f32[16,2]{0,1:T(2,128)} %param.12) | copy-start | bytes 388
  183.1 10.8 %all-to-all-start.1 = ((bf16[4,8,6144]{2,1,0:T(8,128)(2,1)}), bf16[4,8,6144]{2,1,0:T(8,128)(2,1)S(1)}, u32[]{:S(2)}, u32[]{:S(2)}) async-start(bf16[4,8,6144]{2,1,0:T(8,128)(2,1)} %bitcast.36), calls=%async_computation.2 | async-start | bytes 786432 | tf_op jit(solution)/shard_map/all_to_all | solution.py:39
Sparse Core Ops, SparseCore 0:
  22.1 60.6 all-gather.1
  110.1 73.0 reduce-scatter.1
where the time goes:
time: 204 us
  waiting for transfers between devices  141 us (69%)
  matrix products  28.3 us (14%)
  between operations  13.5 us (7%)
  blocking collectives  11.6 us (6%)
  other arithmetic  4.34 us (2%)
  starting transfers between devices  3.5 us (2%)
    reduce_scatter x1, waiting for transfers between devices, local(): lax.psum_scatter(jnp.dot(piece, down_local, preferred_element_type=jnp.fl...  73 us
    all_gather x1, waiting for transfers between devices, local(): lax.all_gather(arrived.reshape(experts * CAP, features), 'mp', axis=0, ti...  60.8 us
    dot_general x1, matrix products, local(): jnp.dot(piece, down_local, preferred_element_type=jnp.float32)  17 us
    all_to_all x1, blocking collectives, local(): lax.all_to_all(outgoing, 'expert', split_axis=0, concat_axis=0, tiled=True)  11.6 us
    dot_general x1, matrix products, local(): gate_proj = jnp.dot(piece, gate_local, preferred_element_type=jnp.float32)  10.1 us
    all_to_all x1, waiting for transfers between devices, local(): lax.all_to_all(results, 'expert', split_axis=0, concat_axis=0, tiled=True)  7.27 us
  transfers between devices with their start and end apart: 3, of which 3 were waited for; matrix products, arithmetic and copies ran while one was open for 0% of the time, Pallas kernels for 0%

commit v1 on v0

v1 whole, which is shorter than its diff:
```python
import functools
import math
import jax
import jax.numpy as jnp
from jax import lax
from jax.experimental import pallas as pl
from jax.experimental.pallas import tpu as pltpu
from jax.sharding import PartitionSpec as P

CAP = 8
LANES = 128
VMEM_BYTES = 67000000
ORDERS = (("x", "y", "z"), ("y", "z", "x"), ("z", "x", "y"))
AXES = ("y", "z", "x")


class Place:
    def __init__(self, dims):
        self.dims = dims
        expert, mp = lax.axis_index("expert"), lax.axis_index("mp")
        self.core = lax.rem(expert, 2)
        self.at = {
            "y": lax.div(expert, 2),
            "z": lax.div(mp, dims["x"]),
            "x": lax.rem(mp, dims["x"]),
        }

    def device(self, axis=None, step=0, core=None):
        at = dict(self.at)
        if axis is not None:
            at[axis] = at[axis] + step
        core = self.core if core is None else core
        return {"expert": at["y"] * 2 + core, "mp": at["z"] * self.dims["x"] + at["x"]}

    def region(self, order, phase, where):
        found = {}
        for turn, axis in enumerate(order):
            if turn < phase:
                found[axis] = pl.ds(0, self.dims[axis])
            elif turn == phase:
                found[axis] = pl.ds(where, 1)
            else:
                found[axis] = pl.ds(self.at[axis], 1)
        return found

    def greet(self):
        barrier = pltpu.get_barrier_semaphore()
        count = 1
        pl.semaphore_signal(
            barrier, inc=1, device_id=self.device(core=1 - self.core),
            device_id_type=pl.DeviceIdType.MESH,
        )
        for axis in AXES:
            for step in (1, -1):
                there = self.inside(axis, self.at[axis] + step)
                count = count + there.astype(jnp.int32)

                @pl.when(there)
                def _():
                    pl.semaphore_signal(
                        barrier, inc=1, device_id=self.device(axis, step),
                        device_id_type=pl.DeviceIdType.MESH,
                    )

        pl.semaphore_wait(barrier, count)

    def inside(self, axis, where):
        return (where >= 0) & (where < self.dims[axis])


def remote(src, dst, send, recv, device):
    return pltpu.make_async_remote_copy(
        src_ref=src, dst_ref=dst, send_sem=send, recv_sem=recv,
        device_id=device, device_id_type=pl.DeviceIdType.MESH,
    )


def messages(dims):
    listed = []
    for phase in range(3):
        for step in range(max(dims.values()) - 1):
            for part, order in enumerate(ORDERS):
                if step < dims[order[phase]] - 1:
                    for way in (1, -1):
                        listed.append((part, phase, order[phase], step, way))
    return listed


def grouped(dims):
    groups = {}
    for number, message in enumerate(messages(dims)):
        groups.setdefault((message[1], message[3]), []).append((number,) + message)
    return groups


def gather_kernel(dims, cuts, x_ref, out_ref, own_sem, send, recv, pair_send, pair_recv):
    me = Place(dims)
    groups = grouped(dims)
    total = len(messages(dims))

    def view(part, found, core):
        first, width = cuts[part]
        return out_ref.at[
            found["y"], pl.ds(core, 1), found["z"], found["x"], :, pl.ds(first, width)
        ]

    mine = out_ref.at[me.at["y"], me.core, me.at["z"], me.at["x"]]
    own = pltpu.make_async_copy(x_ref, mine, own_sem)
    own.start()
    me.greet()
    own.wait()
    other = me.device(core=1 - me.core)
    remote(mine, mine, pair_send.at[total], pair_recv.at[total], other).start()

    def outgoing(number, part, phase, axis, step, way):
        at = me.at[axis]
        go = me.inside(axis, at + way) & me.inside(axis, at - way * step)
        block = view(part, me.region(ORDERS[part], phase, at - way * step), me.core)
        copy = remote(block, block, send.at[number], recv.at[number], me.device(axis, way))
        return go, copy

    def incoming(number, part, phase, axis, step, way, core):
        at = me.at[axis]
        origin = at - way * (step + 1)
        go = me.inside(axis, origin)
        return go, view(part, me.region(ORDERS[part], phase, origin), core)

    for key in sorted(groups):
        for message in groups[key]:
            go, copy = outgoing(*message)
            pl.when(go)(copy.start)
        for message in groups[key]:
            number = message[0]
            go, block = incoming(*message, me.core)

            @pl.when(go)
            def _():
                remote(block, block, send.at[number], recv.at[number], other).wait_recv()
                remote(
                    block, block, pair_send.at[number], pair_recv.at[number], other
                ).start()

    for key in sorted(groups):
        for message in groups[key]:
            number = message[0]
            go, copy = outgoing(*message)
            pl.when(go)(copy.wait_send)
            go, block = incoming(*message, me.core)
            _, landed = incoming(*message, 1 - me.core)

            @pl.when(go)
            def _():
                remote(
                    block, block, pair_send.at[number], pair_recv.at[number], other
                ).wait_send()
                remote(
                    landed, landed, pair_send.at[number], pair_recv.at[number], other
                ).wait_recv()

    theirs = out_ref.at[me.at["y"], 1 - me.core, me.at["z"], me.at["x"]]
    remote(mine, mine, pair_send.at[total], pair_recv.at[total], other).wait_send()
    remote(theirs, theirs, pair_send.at[total], pair_recv.at[total], other).wait_recv()


def scatter_kernel(dims, cuts, x_ref, out_ref, acc, pair, own_sem, send, recv, pair_send,
                   pair_recv, *lands):
    me = Place(dims)
    groups = grouped(dims)
    other = me.device(core=1 - me.core)

    def cut(ref, part):
        return ref.at[:, :, :, :, pl.ds(*cuts[part])]

    def own_copy(part):
        return pltpu.make_async_copy(
            x_ref.at[:, me.core, :, :, :, pl.ds(*cuts[part])], cut(acc, part), own_sem.at[part]
        )

    def pair_copy(part):
        return remote(
            x_ref.at[:, 1 - me.core, :, :, :, pl.ds(*cuts[part])], cut(pair, part),
            pair_send.at[part], pair_recv.at[part], other,
        )

    def add(part, found, land):
        first, width = cuts[part]
        sizes = [found[axis].size for axis in AXES]

        @pl.loop(0, math.prod(sizes))
        def _(unit):
            k = lax.rem(unit, sizes[2])
            j = lax.rem(lax.div(unit, sizes[2]), sizes[1])
            i = lax.div(unit, sizes[2] * sizes[1])
            where = (
                found["y"].start + i, found["z"].start + j, found["x"].start + k,
                slice(None), pl.ds(first, width),
            )
            acc[where] = (
                acc[where].astype(jnp.float32) + land(i, j, k).astype(jnp.float32)
            ).astype(acc.dtype)

    for part in range(3):
        own_copy(part).start()
    me.greet()
    for part in range(3):
        pair_copy(part).start()
    everything = {axis: pl.ds(0, dims[axis]) for axis in AXES}
    for part in range(3):
        own_copy(part).wait()
        pair_copy(part).wait_recv()
        add(part, everything, lambda i, j, k: pair[i, j, k, :, pl.ds(*cuts[part])])

    def outgoing(number, part, phase, axis, step, way):
        at = me.at[axis]
        target = at - way * (step + 1)
        go = me.inside(axis, target)
        found = me.region(ORDERS[part], phase, target)
        block = cut(acc, part).at[found["y"], found["z"], found["x"]]
        return go, remote(
            block, lands[number], send.at[number], recv.at[number], me.device(axis, -way)
        )

    for phase, step in sorted(groups, reverse=True):
        for message in groups[phase, step]:
            go, copy = outgoing(*message)
            pl.when(go)(copy.start)
        for message in groups[phase, step]:
            number, part, _, axis, _, way = message
            at = me.at[axis]
            go = me.inside(axis, at + way) & me.inside(axis, at - way * step)
            found = me.region(ORDERS[part], phase, at - way * step)
            land = lands[number]

            @pl.when(go)
            def _():
                remote(land, land, send.at[number], recv.at[number], other).wait_recv()
                add(part, found, lambda i, j, k: land[i, j, k])

    out_ref[...] = acc[me.at["y"], me.at["z"], me.at["x"]]
    for group in groups.values():
        for message in group:
            go, copy = outgoing(*message)
            pl.when(go)(copy.wait_send)
    for part in range(3):
        pair_copy(part).wait_send()


def axis_dims():
    mp = lax.axis_size("mp")
    along_z = math.gcd(mp, 4)
    return {"y": lax.axis_size("expert") // 2, "z": along_z, "x": mp // along_z}


def column_cuts(columns):
    tiles = columns // LANES
    middle = tiles * 3 // 8
    widths = (tiles - 2 * middle, middle, middle)
    starts = (0, widths[0], widths[0] + widths[1])
    return tuple((a * LANES, b * LANES) for a, b in zip(starts, widths))


def gather_all(payload):
    dims = axis_dims()
    rows, columns = payload.shape
    total = len(messages(dims))
    gathered = pl.pallas_call(
        functools.partial(gather_kernel, dims, column_cuts(columns)),
        out_shape=jax.ShapeDtypeStruct(
            (dims["y"], 2, dims["z"], dims["x"], rows, columns), payload.dtype
        ),
        in_specs=[pl.BlockSpec(memory_space=pl.ANY)],
        out_specs=pl.BlockSpec(memory_space=pltpu.VMEM),
        scratch_shapes=[
            pltpu.SemaphoreType.DMA,
            pltpu.SemaphoreType.DMA((total,)),
            pltpu.SemaphoreType.DMA((total,)),
            pltpu.SemaphoreType.DMA((total + 1,)),
            pltpu.SemaphoreType.DMA((total + 1,)),
        ],
        compiler_params=pltpu.CompilerParams(
            collective_id=0, has_side_effects=True, vmem_limit_bytes=VMEM_BYTES
        ),
        name="token_gather",
    )(payload)
    return gathered.reshape(-1, columns)


def scatter_sum(spread, rows):
    dims = axis_dims()
    columns = spread.shape[1]
    cuts = column_cuts(columns)
    listed = messages(dims)
    lands = []
    for part, phase, axis, step, way in listed:
        done = ORDERS[part][:phase]
        lands.append(
            pltpu.VMEM(
                tuple(dims[a] if a in done else 1 for a in AXES) + (rows, cuts[part][1]),
                spread.dtype,
            )
        )
    whole = (dims["y"], dims["z"], dims["x"], rows, columns)
    return pl.pallas_call(
        functools.partial(scatter_kernel, dims, cuts),
        out_shape=jax.ShapeDtypeStruct((rows, columns), spread.dtype),
        in_specs=[pl.BlockSpec(memory_space=pl.ANY)],
        out_specs=pl.BlockSpec(memory_space=pltpu.VMEM),
        scratch_shapes=[
            pltpu.VMEM(whole, spread.dtype),
            pltpu.VMEM(whole, spread.dtype),
            pltpu.SemaphoreType.DMA((3,)),
            pltpu.SemaphoreType.DMA((len(listed),)),
            pltpu.SemaphoreType.DMA((len(listed),)),
            pltpu.SemaphoreType.DMA((3,)),
            pltpu.SemaphoreType.DMA((3,)),
        ]
        + lands,
        compiler_params=pltpu.CompilerParams(
            collective_id=1, has_side_effects=True, vmem_limit_bytes=VMEM_BYTES
        ),
        name="result_scatter",
    )(spread.reshape(dims["y"], 2, dims["z"], dims["x"], rows, columns))


def local(tokens, norm_gain, expert_ids, slot_ids, route_weights, w_gate, w_up, w_down):
    tok_rows, features = tokens.shape
    blocks = lax.axis_size("expert") * lax.axis_size("mp")
    values = tokens.astype(jnp.float32)
    mean_square = jnp.mean(values * values, axis=1, keepdims=True)
    normed = (values * lax.rsqrt(mean_square + 1e-05) * norm_gain.astype(jnp.float32)).astype(
        jnp.bfloat16
    )
    shares = route_weights / (route_weights[:, 0:1] + route_weights[:, 1:2])
    share_hi = shares.astype(jnp.bfloat16)
    share_lo = (shares - share_hi.astype(jnp.float32)).astype(jnp.bfloat16)
    info = jnp.concatenate(
        [expert_ids.astype(jnp.bfloat16), slot_ids.astype(jnp.bfloat16), share_hi, share_lo], axis=1
    )
    info = jnp.pad(info, ((0, 0), (0, 128 - info.shape[1])))
    payload = jnp.concatenate([normed, info], axis=1)
    gathered = gather_all(payload)
    everyone = gathered[:, :features]
    table = gathered[:, features:].astype(jnp.float32)
    ids = table[:, 0:2].astype(jnp.int32)
    slots = table[:, 2:4].astype(jnp.int32)
    weights = table[:, 4:6] + table[:, 6:8]
    total = blocks * tok_rows
    block = lax.broadcasted_iota(jnp.int32, (total, 2), 0) // tok_rows
    place = jnp.where(ids == lax.axis_index("expert"), block * CAP + slots, -1)
    rows = lax.broadcasted_iota(jnp.int32, (blocks * CAP, total), 0)
    hit0 = rows == place[None, :, 0]
    hit1 = rows == place[None, :, 1]
    placing = (hit0 | hit1).astype(jnp.bfloat16)
    row_weight = jnp.sum(
        jnp.where(hit0, weights[None, :, 0], 0.0) + jnp.where(hit1, weights[None, :, 1], 0.0),
        axis=1,
        keepdims=True,
    )
    piece = jnp.dot(placing, everyone, preferred_element_type=jnp.float32).astype(jnp.bfloat16)
    gate_proj = jnp.dot(piece, w_gate[0], preferred_element_type=jnp.float32)
    up_proj = jnp.dot(piece, w_up[0], preferred_element_type=jnp.float32)
    hidden = (jax.nn.silu(gate_proj) * up_proj).astype(jnp.bfloat16)
    part = jnp.dot(hidden, w_down[0], preferred_element_type=jnp.float32)
    part = (part * row_weight).astype(jnp.bfloat16)
    spread = lax.dot_general(
        placing, part, (((0,), (0,)), ((), ())), preferred_element_type=jnp.float32
    ).astype(jnp.bfloat16)
    return scatter_sum(spread, tok_rows)


def solution(mesh):
    placed = (
        P(("expert", "mp"), None),
        P(),
        P(("expert", "mp"), None),
        P(("expert", "mp"), None),
        P(("expert", "mp"), None),
        P("expert", None, "mp"),
        P("expert", None, "mp"),
        P("expert", "mp", None),
    )
    return jax.shard_map(
        local, mesh=mesh, in_specs=placed, out_specs=P(("expert", "mp"), None), check_vma=False
    )
```

time: 204 us -> 147 us (0.72)
  waiting for transfers between devices: 141 us -> 0 us
  Pallas kernels: 0 us -> 103 us
  between operations: 13.5 us -> 0.12 us
  blocking collectives: 11.6 us -> 0 us
  matrix products: 28.3 us -> 32.7 us
  local copies, waits for them, and re-layouts: 1.54 us -> 5.27 us
  starting transfers between devices: 3.5 us -> 0 us
    pallas_call x0 -> x2, Pallas kernels: none -> 103 us  [the longest x1 54 us: scatter_sum(): pl.pallas_call(functools.partial(scatter_kernel, dims, cuts), out_shape=j...]
    reduce_scatter x1 -> x0, waiting for transfers between devices: 73 us -> none  [local(): lax.psum_scatter(jnp.dot(piece, down_local, preferred_element_type=jnp.fl...]
    all_gather x1 -> x0, waiting for transfers between devices: 60.8 us -> none  [local(): lax.all_gather(arrived.reshape(experts * CAP, features), 'mp', axis=0, ti...]
    all_to_all x1 -> x0, blocking collectives: 11.6 us -> none  [local(): lax.all_to_all(outgoing, 'expert', split_axis=0, concat_axis=0, tiled=True)]
    all_to_all x1 -> x0, waiting for transfers between devices: 7.27 us -> none  [local(): lax.all_to_all(results, 'expert', split_axis=0, concat_axis=0, tiled=True)]
    dot_general x3 -> x4, matrix products: 28.3 us -> 32.7 us  [the longest x1 16.1 us: local(): part = jnp.dot(hidden, w_down[0], preferred_element_type=jnp.float32)]
    unnamed x4 -> x5, local copies, waits for them, and re-layouts: 0.01 us -> 4.14 us
    all_to_all x1 -> x0, starting transfers between devices: 3.46 us -> none  [local(): lax.all_to_all(results, 'expert', split_axis=0, concat_axis=0, tiled=True)]
  transfers between devices with their start and end apart: 3 -> 0, of which waited for: 3 -> 0; matrix products, arithmetic and copies ran while one was open for 0% -> 0% of each run, Pallas kernels for 0% -> 0%
where the time goes in v1:
time: 147 us
  Pallas kernels  103 us (70%)
  matrix products  32.7 us (22%)
  other arithmetic  6.07 us (4%)
  local copies, waits for them, and re-layouts  5.27 us (4%)
    pallas_call x1, Pallas kernels, scatter_sum(): pl.pallas_call(functools.partial(scatter_kernel, dims, cuts), out_shape=j...  54 us
    pallas_call x1, Pallas kernels, gather_all(): pl.pallas_call(functools.partial(gather_kernel, dims, column_cuts(columns...  48.8 us
    dot_general x1, matrix products, local(): part = jnp.dot(hidden, w_down[0], preferred_element_type=jnp.float32)  16.1 us
    dot_general x1, matrix products, local(): gate_proj = jnp.dot(piece, w_gate[0], preferred_element_type=jnp.float32)  7.42 us
    dot_general x1, matrix products, local(): jnp.dot(placing, everyone, preferred_element_type=jnp.float32)  4.59 us
    dot_general x1, matrix products, local(): lax.dot_general(placing, part, (((0,), (0,)), ((), ())), preferred_elemen...  4.53 us
    unnamed x5, local copies, waits for them, and re-layouts  4.14 us

profile of v1, /device:TPU:0, one launch (start us, length us, event | category | flops | bytes accessed | tf_op | source)
XLA Modules:
  0.0 146.9 jit_solution(4422526927421139020)
XLA Ops:
  0.0 0.8 copy.20
  0.8 0.8 add_bitcast_fusion
  1.5 0.1 fusion.40
  1.6 0.7 convert_element_type.51
  2.3 0.1 copy.22
  2.4 0.7 convert_element_type.52
  3.1 0.1 copy.23
  3.2 0.1 fusion.35
  3.2 0.7 convert_element_type.49
  4.0 1.1 fusion.22
  5.1 1.0 fusion.24
  6.1 0.7 pad_maximum_fusion.x_ref
  6.8 48.8 %token_gather.1 = bf16[2,2,4,2,16,6272]{5,4,3,2,1,0:T(8,128)(2,1)} custom-call(bf16[16,6272]{1,0:T(8,128)(2,1)} %pad_maximum_fusion.x_ref), custom_call_target="tpu_custom_call" | custom-call | tf_op jit(solution)/shard_map/token_gather/pallas_call | solution.py:266
  55.6 0.9 slice.48
  56.5 0.1 copy.25
  56.7 0.2 add_reduce_fusion
  56.9 4.6 %convolution_convert_fusion.1 = bf16[256,6144]{1,0:T(8,128)(2,1)S(1)} fusion(bf16[512,6272]{1,0:T(8,128)(2,1)} %bitcast.39, s32[512]{0:T(512)S(1)} %bitcast.44, s32[512]{0:T(512)S(1)} %bitcast.41), kind=kOutput, calls=%fused_computation.9 | convolution fusion | flops 1612578816 | bytes 9441280 | tf_op jit(solution)/shard_map/dot_general | solution.py:359
  61.5 0.0 copy-start
  61.5 1.7 %copy-done = bf16[256,6144]{1,0:T(8,128)(2,1)} copy-done((bf16[256,6144]{1,0:T(8,128)(2,1)}, bf16[256,6144]{1,0:T(8,128)(2,1)S(1)}, u32[]{:S(2)}) %copy-start) | copy-done | bytes 3145752
  63.2 7.4 %fusion.4 = f32[256,1024]{1,0:T(8,128)} fusion(bf16[256,6144]{1,0:T(8,128)(2,1)S(1)} %convolution_convert_fusion.1, bf16[1,6144,1024]{2,1,0:T(8,128)(2,1)} %param.13), kind=kOutput, calls=%fused_computation.4 | convolution fusion | flops 3221225472 | bytes 16777216 | tf_op jit(solution)/shard_map/dot_general | solution.py:360
  70.6 16.1 %fusion.9 = bf16[256,6144]{1,0:T(8,128)(2,1)S(1)} fusion(bf16[1,1024,6144]{2,1,0:T(8,128)(2,1)} %param.15, f32[256]{0:T(256)S(1)} %add_reduce_fusion, bf16[256,6144]{1,0:T(8,128)(2,1)} %copy-done, bf16[1,6144,1024]{2,1,0:T(8,128)(2,1)} %param.14, f32[256,1024]{1,0:T(8,128)} %fusion.4), kind=kOutput, calls=%fused_computation.8 | convolution fusion | flops 6447169536 | bytes 32506880 | tf_op jit(solution)/shard_map/dot_general | solution.py:363
  86.7 4.5 %convolution_convert_fusion = bf16[512,6144]{1,0:T(8,128)(2,1)} fusion(bf16[256,6144]{1,0:T(8,128)(2,1)S(1)} %fusion.9, s32[512]{0:T(512)S(1)} %bitcast.45, s32[512]{0:T(512)S(1)} %bitcast.42), kind=kOutput, calls=%fused_computation.6 | convolution fusion | flops 1614151680 | bytes 9441280 | tf_op jit(solution)/shard_map/dot_general | solution.py:365
  91.3 54.0 %result_scatter.1 = bf16[16,6144]{1,0:T(8,128)(2,1)} custom-call(bf16[2,2,4,2,16,6144]{5,4,3,2,1,0:T(8,128)(2,1)} %bitcast.37), custom_call_target="tpu_custom_call" | custom-call | tf_op jit(solution)/shard_map/result_scatter/pallas_call | solution.py:303
  145.2 1.6 %copy.27 = bf16[16,6144]{1,0:T(8,128)(2,1)} copy(bf16[16,6144]{1,0:T(8,128)(2,1)} %result_scatter.1) | data formatting | bytes 393216
  (8 shorter events, 0.1 us)
Async XLA Ops:
  61.5 1.7 %copy-start = (bf16[256,6144]{1,0:T(8,128)(2,1)}, bf16[256,6144]{1,0:T(8,128)(2,1)S(1)}, u32[]{:S(2)}) copy-start(bf16[256,6144]{1,0:T(8,128)(2,1)S(1)} %convolution_convert_fusion.1) | copy-start | bytes 9437188
